TPU v7x, 32 devices: a whole 2x2x4 slice. The times are simulated.
32 devices in a mesh: rep: 4 (over x, y), dp: 8 (over z, core).
Axes of the slice: x: 2, y: 2, z: 4, core: 2. Of those that a mesh axis runs over, the one named last changes fastest.
Arguments:
- x: bfloat16 [32, 2048, 1024], P(('rep', 'dp')), parts along dimension 0
- dy: bfloat16 [32, 2048, 1024], P(('rep', 'dp')), parts along dimension 0
- w_gate: bfloat16 [2, 1024, 4096], replicated
- w_up: bfloat16 [2, 1024, 4096], replicated
- w_down: bfloat16 [2, 4096, 1024], replicated
- m_w_gate: float32 [2, 1024, 4096], P(None, 'dp')
- m_w_up: float32 [2, 1024, 4096], P(None, 'dp')
- m_w_down: float32 [2, 4096, 1024], P(None, 'dp')
- v_w_gate: float32 [2, 1024, 4096], P(None, 'dp')
- v_w_up: float32 [2, 1024, 4096], P(None, 'dp')
- v_w_down: float32 [2, 4096, 1024], P(None, 'dp')
Outputs:
- output 1: bfloat16 [8, 1024, 4096], P('rep'), parts along dimension 0
- output 2: bfloat16 [8, 1024, 4096], P('rep'), parts along dimension 0
- output 3: bfloat16 [8, 4096, 1024], P('rep'), parts along dimension 0
- output 4: float32 [8, 1024, 4096], P('rep', 'dp'), parts along dimension 0
- output 5: float32 [8, 1024, 4096], P('rep', 'dp'), parts along dimension 0
- output 6: float32 [8, 4096, 1024], P('rep', 'dp'), parts along dimension 0
- output 7: float32 [8, 1024, 4096], P('rep', 'dp'), parts along dimension 0
- output 8: float32 [8, 1024, 4096], P('rep', 'dp'), parts along dimension 0
- output 9: float32 [8, 4096, 1024], P('rep', 'dp'), parts along dimension 0
There are 4 independent parts. A program takes and returns all parts, laid end to end along the dimension named above; an argument that names none is the same for every part.
All inputs are finite; a program needn't handle non-finite values.
Results may differ from a plain program's by a relative error of at most 0.022.
Values are sent between devices in bfloat16 or wider.
A program may use at most 2 GiB of HBM per device.

v0:
```python
import jax
import jax.numpy as jnp
from jax import lax

NAMES = ("w_gate", "w_up", "w_down")


def matmul(a, w):
    return jnp.dot(a, w, preferred_element_type=jnp.float32).astype(jnp.bfloat16)


def normed(h):
    wide = h.astype(jnp.float32)
    scale = lax.rsqrt(jnp.mean(wide**2, -1, keepdims=True) + 1e-6)
    return (wide * scale).astype(jnp.bfloat16)


def layer(h, w):
    a = normed(h)
    gate = jnp.dot(a, w["w_gate"], preferred_element_type=jnp.float32)
    up = jnp.dot(a, w["w_up"], preferred_element_type=jnp.float32)
    return h + matmul((jax.nn.silu(gate) * up).astype(jnp.bfloat16), w["w_down"])


def adamw(w, m, v, g):
    m = 0.9 * m + 0.1 * g
    v = 0.95 * v + 0.05 * g * g
    step = m * lax.rsqrt(v + 1e-8) + 0.1 * w
    return (w - 0.02 * step).astype(jnp.bfloat16), m, v


def stack(weights, h):
    for number in range(weights["w_gate"].shape[0]):
        h = layer(h, {name: w[number] for name, w in weights.items()})
    return h


def solution(mesh):
    groups = mesh.shape["rep"]

    def step(x, dy, *arrays):
        weights, m, v = (arrays[i : i + 3] for i in (0, 3, 6))
        x, dy = (t.reshape(groups, -1, *t.shape[1:]) for t in (x, dy))

        def of_a_group(x, dy):
            _, back = jax.vjp(lambda w: stack(w, x), dict(zip(NAMES, weights, strict=True)))
            by_weights = back(dy)[0]
            gradients = [by_weights[name].astype(jnp.float32) for name in NAMES]
            new = [adamw(w.astype(jnp.float32), m, v, g) for w, m, v, g in zip(weights, m, v, gradients, strict=True)]
            return tuple(one[which] for which in range(3) for one in new)

        return tuple(t.reshape(-1, *t.shape[2:]) for t in jax.vmap(of_a_group)(x, dy))

    return step
```

profile of v0, /device:TPU:0, one launch (start us, length us, event | category | flops | bytes accessed | tf_op | source)
XLA Modules:
  0.0 1710.5 jit_solution(8692154925177402)
XLA Ops:
  16.8 24.6 %fusion.67 = f32[2048,4096]{1,0:T(8,128)} fusion(bf16[2,1024,4096]{2,1,0:T(8,128)(2,1)} %param, bf16[1,2048,1024]{2,1,0:T(8,128)(2,1)} %param.2, f32[2048]{0:T(1024)S(1)} %add_rsqrt_fusion), kind=kOutput, calls=%fused_computation.78 | convolution fusion | flops 17186160640 | bytes 46145536 | tf_op jit(solution)/vmap(jvp())/dot_general | solution.py:20
  41.3 23.4 %fusion.65 = f32[2048,4096]{1,0:T(8,128)} fusion(bf16[2,1024,4096]{2,1,0:T(8,128)(2,1)} %param.3, bf16[1,2048,1024]{2,1,0:T(8,128)(2,1)S(1)} %copy-done.2, f32[2048]{0:T(1024)S(1)} %add_rsqrt_fusion), kind=kOutput, calls=%fused_computation.76 | convolution fusion | flops 17186160640 | bytes 46145536 | tf_op jit(solution)/vmap(jvp())/dot_general | solution.py:21
  64.8 27.5 %fusion.26 = bf16[2048,4096]{1,0:T(8,128)(2,1)} fusion(f32[2048,4096]{1,0:T(8,128)} %fusion.65, f32[2048,4096]{1,0:T(8,128)} %fusion.67), kind=kLoop, calls=%fused_computation.35 | loop fusion | flops 50331648 | bytes 83886080
  92.3 24.0 %fusion.51 = (f32[2048]{0:T(1024)S(1)}, bf16[1,1,2048,1024]{2,3,1,0:T(8,128)(2,1)S(1)}) fusion(bf16[2048,4096]{1,0:T(8,128)(2,1)} %fusion.26, bf16[2,4096,1024]{2,1,0:T(8,128)(2,1)} %param.4, bf16[1,2048,1024]{1,2,0:T(8,128)(2,1)} %copy), kind=kOutput, calls=%fused_computation.62 | convolution fusion | flops 17190352896 | bytes 33562624 | tf_op jit(solution)/vmap(jvp())/dot_general | solution.py:9
  117.0 24.1 %fusion.54 = f32[2048,4096]{1,0:T(8,128)} fusion(bf16[2,1024,4096]{2,1,0:T(8,128)(2,1)} %param, bf16[1,1,2048,1024]{2,3,1,0:T(8,128)(2,1)S(1)} %get-tuple-element.10, f32[2048]{0:T(1024)S(1)} %bitcast.337), kind=kOutput, calls=%fused_computation.65 | convolution fusion | flops 17186160640 | bytes 46145536 | tf_op jit(solution)/vmap(jvp())/dot_general | solution.py:20
  141.1 23.5 %fusion.58 = f32[2048,4096]{1,0:T(8,128)} fusion(bf16[2,1024,4096]{2,1,0:T(8,128)(2,1)} %param.3, bf16[1,1,2048,1024]{2,3,1,0:T(8,128)(2,1)S(1)} %get-tuple-element.10, f32[2048]{0:T(1024)S(1)} %bitcast.338), kind=kOutput, calls=%fused_computation.69 | convolution fusion | flops 17186160640 | bytes 46145536 | tf_op jit(solution)/vmap(jvp())/dot_general | solution.py:21
  164.6 32.1 %fusion.35 = f32[1,4096,1024]{2,1,0:T(8,128)} fusion(f32[2048,4096]{1,0:T(8,128)} %fusion.58, f32[2048,4096]{1,0:T(8,128)} %fusion.54, bf16[1,2048,1024]{2,1,0:T(8,128)(2,1)} %param.5), kind=kOutput, calls=%fused_computation.52 | convolution fusion | flops 17230200832 | bytes 88080384 | tf_op jit(solution)/vmap(transpose(jvp()))/dot_general | solution.py:9
  203.5 24.4 %convolution_convert_fusion.1 = bf16[2048,4096]{1,0:T(8,128)(2,1)} fusion(bf16[2,4096,1024]{2,1,0:T(8,128)(2,1)} %param.4, bf16[1,2048,1024]{2,1,0:T(8,128)(2,1)} %param.5), kind=kOutput, calls=%fused_computation.44 | convolution fusion | flops 17188257792 | bytes 29360128 | tf_op jit(solution)/vmap(transpose(jvp()))/dot_general | solution.py:9
  227.8 32.9 %fusion.6 = bf16[2048,4096]{1,0:T(8,128)(2,1)} fusion(f32[2048,4096]{1,0:T(8,128)} %fusion.54, f32[2048,4096]{1,0:T(8,128)} %fusion.58, bf16[2048,4096]{1,0:T(8,128)(2,1)} %convolution_convert_fusion.1), kind=kLoop, calls=%fused_computation.11 | loop fusion | flops 100663296 | bytes 100663296
  260.7 26.9 %fusion.24 = bf16[2048,1024]{0,1:T(8,128)(2,1)} fusion(bf16[2048,4096]{1,0:T(8,128)(2,1)} %convolution_convert_fusion.1, f32[2048,4096]{1,0:T(8,128)} %fusion.54, bf16[2,1024,4096]{2,1,0:T(8,128)(2,1)} %param.3), kind=kOutput, calls=%fused_computation.34 | convolution fusion | flops 17230200832 | bytes 62914560 | tf_op jit(solution)/vmap(transpose(jvp()))/dot_general | solution.py:21
  287.7 25.0 %fusion.53 = (f32[2048]{0:T(1024)S(1)}, bf16[2048,1024]{0,1:T(8,128)(2,1)S(1)}) fusion(bf16[1,1,2048,1024]{2,3,1,0:T(8,128)(2,1)} %copy-done.3, bf16[2048,1024]{0,1:T(8,128)(2,1)} %fusion.24, bf16[2048,4096]{1,0:T(8,128)(2,1)} %fusion.6, bf16[2,1024,4096]{2,1,0:T(8,128)(2,1)} %param), kind=kOutput, calls=%fused_computation.64 | convolution fusion | flops 17190352896 | bytes 37756928 | tf_op jit(solution)/vmap(transpose(jvp()))/dot_general | solution.py:20
  340.3 23.7 %convolution_bitcast_fusion.1 = f32[1,1024,4096]{2,1,0:T(8,128)} fusion(bf16[2048,4096]{1,0:T(8,128)(2,1)} %fusion.6, bf16[1,1,2048,1024]{2,3,1,0:T(8,128)(2,1)} %copy-done.3, f32[2048]{0:T(1024)S(1)} %bitcast.340), kind=kOutput, calls=%fused_computation.57 | convolution fusion | flops 17186160640 | bytes 37756928 | tf_op jit(solution)/vmap(transpose(jvp()))/dot_general | solution.py:20
  364.1 24.8 %convolution_convert_fusion = bf16[2048,4096]{1,0:T(8,128)(2,1)} fusion(bf16[2048,1024]{0,1:T(8,128)(2,1)} %copy-done.5, bf16[2,4096,1024]{2,1,0:T(8,128)(2,1)} %param.4), kind=kOutput, calls=%fused_computation.43 | convolution fusion | flops 17188257792 | bytes 29360128 | tf_op jit(solution)/vmap(transpose(jvp()))/dot_general | solution.py:9
  388.9 39.0 %fusion.41 = f32[1,1024,4096]{2,1,0:T(8,128)} fusion(f32[2048,4096]{1,0:T(8,128)} %fusion.67, f32[2048,4096]{1,0:T(8,128)} %fusion.65, bf16[2048,4096]{1,0:T(8,128)(2,1)} %convolution_convert_fusion, bf16[1,2048,1024]{1,2,0:T(8,128)(2,1)} %copy, f32[2048]{0:T(1024)S(1)} %copy-done.11), kind=kOutput, calls=%fused_computation.54 | convolution fusion | flops 17278435328 | bytes 104865792 | tf_op jit(solution)/vmap(transpose(jvp()))/dot_general | solution.py:20
  428.0 29.4 %fusion.38 = f32[1,1024,4096]{2,1,0:T(8,128)} fusion(bf16[2048,4096]{1,0:T(8,128)(2,1)} %convolution_convert_fusion.1, f32[2048,4096]{1,0:T(8,128)} %fusion.54, bf16[1,1,2048,1024]{2,3,1,0:T(8,128)(2,1)} %copy-done.3, f32[2048]{0:T(1024)S(1)} %bitcast.341), kind=kOutput, calls=%fused_computation.53 | convolution fusion | flops 17236492288 | bytes 71311360 | tf_op jit(solution)/vmap(transpose(jvp()))/dot_general | solution.py:21
  457.5 29.6 %fusion.44 = f32[1,1024,4096]{2,1,0:T(8,128)} fusion(bf16[2048,4096]{1,0:T(8,128)(2,1)} %convolution_convert_fusion, f32[2048,4096]{1,0:T(8,128)} %fusion.67, bf16[1,2048,1024]{1,2,0:T(8,128)(2,1)} %copy, f32[2048]{0:T(1024)S(1)} %copy-done.11), kind=kOutput, calls=%fused_computation.55 | convolution fusion | flops 17236492288 | bytes 71311360 | tf_op jit(solution)/vmap(transpose(jvp()))/dot_general | solution.py:21
  490.8 46.0 %reduce-scatter.29.cloned.1.call-done = f32[1,512,1024]{2,1,0:T(8,128)} async-done(((f32[1,4096,1024]{2,1,0:T(8,128)}), f32[1,512,1024]{2,1,0:T(8,128)}) %reduce-scatter.29.cloned.1.call-update) | async-done | bytes 2097168
  546.4 159.6 %reduce-scatter.19.cloned.1.call-done = f32[1,128,4096]{2,1,0:T(8,128)} async-done(((f32[1,1024,4096]{2,1,0:T(8,128)}), f32[1,128,4096]{2,1,0:T(8,128)}) %reduce-scatter.19.cloned.1.call-update) | async-done | bytes 2097168
  707.7 167.9 %reduce-scatter.21.cloned.1.call-done = f32[1,128,4096]{2,1,0:T(8,128)} async-done(((f32[1,1024,4096]{2,1,0:T(8,128)}), f32[1,128,4096]{2,1,0:T(8,128)}) %reduce-scatter.21.cloned.1.call-update) | async-done | bytes 2097168
  885.0 159.6 %reduce-scatter.23.cloned.1.call-done = f32[1,128,4096]{2,1,0:T(8,128)} async-done(((f32[1,1024,4096]{2,1,0:T(8,128)}), f32[1,128,4096]{2,1,0:T(8,128)}) %reduce-scatter.23.cloned.1.call-update) | async-done | bytes 2097168
  1046.3 167.9 %reduce-scatter.25.cloned.1.call-done = f32[1,128,4096]{2,1,0:T(8,128)} async-done(((f32[1,1024,4096]{2,1,0:T(8,128)}), f32[1,128,4096]{2,1,0:T(8,128)}) %reduce-scatter.25.cloned.1.call-update) | async-done | bytes 2097168
  1223.5 142.0 %all-gather.14.cloned.1.call-done = bf16[1,2,4096,1024]{3,2,1,0:T(8,128)(2,1)} async-done(((bf16[1,2,512,1024]{3,2,1,0:T(8,128)(2,1)}), bf16[1,2,4096,1024]{3,2,1,0:T(8,128)(2,1)}) %all-gather.14.cloned.1.call-update) | async-done | bytes 16777232 | tf_op jit(solution)/reshape | solution.py:52
  1365.5 151.9 %all-gather.10.cloned.1.call-done = bf16[1,2,1024,4096]{3,2,1,0:T(8,128)(2,1)} async-done(((bf16[1,2,128,4096]{3,2,1,0:T(8,128)(2,1)}), bf16[1,2,1024,4096]{3,2,1,0:T(8,128)(2,1)}) %all-gather.10.cloned.1.call-update) | async-done | bytes 16777232 | tf_op jit(solution)/reshape | solution.py:52
  1517.5 152.0 %all-gather.12.cloned.1.call-done = bf16[1,2,1024,4096]{3,2,1,0:T(8,128)(2,1)} async-done(((bf16[1,2,128,4096]{3,2,1,0:T(8,128)(2,1)}), bf16[1,2,1024,4096]{3,2,1,0:T(8,128)(2,1)}) %all-gather.12.cloned.1.call-update) | async-done | bytes 16777232 | tf_op jit(solution)/reshape | solution.py:52
  (76 shorter events, 113.5 us)
Async XLA Ops:
  7.2 481.9 %reduce-scatter.27.cloned.1.call-start = ((), (), s32[]{:S(2)}) async-start(), calls=%async_computation.13 | async-start | bytes 18874368
  16.7 24.6 %copy-start.10 = (f32[2048]{0:T(1024)}, f32[2048]{0:T(1024)S(1)}, u32[]{:S(2)}) copy-start(f32[2048]{0:T(1024)S(1)} %add_rsqrt_fusion) | copy-start | bytes 24580
  16.7 24.6 %copy-start.2 = (bf16[1,2048,1024]{2,1,0:T(8,128)(2,1)S(1)}, bf16[1,2048,1024]{2,1,0:T(8,128)(2,1)}, u32[]{:S(2)}) copy-start(bf16[1,2048,1024]{2,1,0:T(8,128)(2,1)} %param.2) | copy-start | bytes 12582916
  116.3 24.8 %copy-start.3 = (bf16[1,1,2048,1024]{2,3,1,0:T(8,128)(2,1)}, bf16[1,1,2048,1024]{2,3,1,0:T(8,128)(2,1)S(1)}, u32[]{:S(2)}) copy-start(bf16[1,1,2048,1024]{2,3,1,0:T(8,128)(2,1)S(1)} %get-tuple-element.10) | copy-start | bytes 12582916
  117.0 24.1 %copy-start.8 = (f32[1,1,2048]{2,1,0:T(1,128)}, f32[1,1,2048]{2,1,0:T(1,128)S(1)}, u32[]{:S(2)}) copy-start(f32[1,1,2048]{2,1,0:T(1,128)S(1)} %rsqrt.31) | copy-start | bytes 24580
  196.8 340.0 %reduce-scatter.29.cloned.1.call-start = ((), (), s32[]{:S(2)}) async-start(), calls=%async_computation.14 | async-start | bytes 18874368
  287.6 25.0 %copy-start.7 = (f32[2048]{0:T(1024)S(1)}, f32[2048]{0:T(1024)}, u32[]{:S(2)}) copy-start(f32[2048]{0:T(1024)} %copy-done.6) | copy-start | bytes 24580
  287.6 25.1 %copy-start = (bf16[1,2048,1024]{1,2,0:T(8,128)(2,1)S(1)}, bf16[1,2048,1024]{1,2,0:T(8,128)(2,1)}, u32[]{:S(2)}) copy-start(bf16[1,2048,1024]{1,2,0:T(8,128)(2,1)} %copy.1) | copy-start | bytes 12582916
  287.6 25.1 %copy-start.4 = (bf16[1,1,2048,1024]{2,3,1,0:T(8,128)(2,1)S(1)}, bf16[1,1,2048,1024]{2,3,1,0:T(8,128)(2,1)}, u32[]{:S(2)}) copy-start(bf16[1,1,2048,1024]{2,3,1,0:T(8,128)(2,1)} %copy-done.3) | copy-start | bytes 12582916
  287.7 25.1 %copy-start.9 = (f32[1,1,2048]{2,1,0:T(1,128)S(1)}, f32[1,1,2048]{2,1,0:T(1,128)}, u32[]{:S(2)}) copy-start(f32[1,1,2048]{2,1,0:T(1,128)} %copy-done.8) | copy-start | bytes 24580
  315.9 2.0 copy-start.5
  340.3 365.7 %reduce-scatter.19.cloned.1.call-start = ((), (), s32[]{:S(2)}) async-start(), calls=%async_computation.9 | async-start | bytes 18874368
  364.1 24.9 %copy-start.11 = (f32[2048]{0:T(1024)S(1)}, f32[2048]{0:T(1024)}, u32[]{:S(2)}) copy-start(f32[2048]{0:T(1024)} %copy-done.10) | copy-start | bytes 24580
  364.1 511.5 %reduce-scatter.21.cloned.1.call-start = ((), (), s32[]{:S(2)}) async-start(), calls=%async_computation.10 | async-start | bytes 18874368
  428.0 616.6 %reduce-scatter.23.cloned.1.call-start = ((), (), s32[]{:S(2)}) async-start(), calls=%async_computation.11 | async-start | bytes 18874368
  457.5 756.6 %reduce-scatter.25.cloned.1.call-start = ((), (), s32[]{:S(2)}) async-start(), calls=%async_computation.12 | async-start | bytes 18874368
  487.2 878.3 %all-gather.14.cloned.1.call-start = ((), (), s32[]{:S(2)}) async-start(), calls=%async_computation.8 | async-start | bytes 18874368 | tf_op jit(solution)/reshape | solution.py:52
  546.3 971.2 %all-gather.10.cloned.1.call-start = ((), (), s32[]{:S(2)}) async-start(), calls=%async_computation.6 | async-start | bytes 18874368 | tf_op jit(solution)/reshape | solution.py:52
  884.9 784.5 %all-gather.12.cloned.1.call-start = ((), (), s32[]{:S(2)}) async-start(), calls=%async_computation.7 | async-start | bytes 18874368 | tf_op jit(solution)/reshape | solution.py:52
  1669.4 16.8 copy-start.1
  1669.4 25.3 %slice-start = ((s8[16777216]{0:T(1024)(128)(4,1)}), s8[4194304]{0:T(1024)(128)(4,1)S(1)}, s32[]{:S(2)}) async-start(s8[16777216]{0:T(1024)(128)(4,1)} %bitcast.329), calls=%async_computation.15 | async-start | bytes 8388608
  1669.4 25.3 %slice-start.1 = ((s8[16777216]{0:T(1024)(128)(4,1)}), s8[4194304]{0:T(1024)(128)(4,1)S(1)}, s32[]{:S(2)}) async-start(s8[16777216]{0:T(1024)(128)(4,1)} %bitcast.329), calls=%async_computation.16 | async-start | bytes 8388608
  1686.2 9.9 slice-start.2
  1686.2 11.1 slice-start.3
  (2 other events, 1.3 us)
Sparse Core Ops, SparseCore 0:
  196.9 170.7 reduce-scatter.26
  370.0 166.7 reduce-scatter.28
  539.2 166.7 reduce-scatter.18
  708.7 166.7 reduce-scatter.20
  877.7 166.7 reduce-scatter.22
  1047.3 166.7 reduce-scatter.24
  1215.7 149.7 all-gather.13
  1367.7 149.7 all-gather.9
  1519.6 149.7 all-gather.11
where the time goes:
time: 1720 us; the launch traced here: 1710 us
  waiting for transfers between devices  1150 us (67%)
  matrix products  397 us (23%)
  other arithmetic  100 us (6%)
  local copies, waits for them, and re-layouts  51 us (3%)
    unnamed x15, waiting for transfers between devices  701 us
    reshape x3, waiting for transfers between devices, step(): t.reshape(-1, *t.shape[2:])  446 us
    dot_general x5, matrix products, layer(): gate = jnp.dot(a, w['w_gate'], preferred_element_type=jnp.float32)  136 us
    dot_general x5, matrix products, layer(): up = jnp.dot(a, w['w_up'], preferred_element_type=jnp.float32)  133 us
    dot_general x5, matrix products, matmul(): jnp.dot(a, w, preferred_element_type=jnp.float32).astype(jnp.bfloat16)  128 us
    unnamed x4, other arithmetic  63.6 us
    unnamed x39, local copies, waits for them, and re-layouts  50.4 us
  transfers between devices with their start and end apart: 9, of which 8 were waited for; matrix products, arithmetic and copies ran while one was open for 19% of the time, Pallas kernels for 0%

commit v1 on v0

v1 whole, which is shorter than its diff:
```python
import functools

import jax
import jax.numpy as jnp
from jax import lax
from jax.experimental import pallas as pl
from jax.experimental.pallas import tpu as pltpu
from jax.sharding import PartitionSpec as P

MESH = pl.DeviceIdType.MESH
T, D, FF = 2048, 1024, 4096
CHIPS = 4
OWNERS = 8
W = 128
TILE = 1024
UNITS = 24
STEPS = 24
TILES = 8
VMEM_LIMIT = 63 << 20
WAYS = (0, 1)
ALONG = ((1,), (1,))
F32, BF16 = jnp.float32, jnp.bfloat16


def normed(wide):
    return (wide * lax.rsqrt(jnp.mean(wide * wide, -1, keepdims=True) + 1e-6)).astype(BF16)


def dot(a, b, dims=((1,), (0,))):
    return lax.dot_general(a, b, (dims, ((), ())), preferred_element_type=F32)


def main(
    x_hbm, dy_hbm, wg_hbm, wu_hbm, wd_hbm, mg_hbm, mu_hbm, md_hbm, vg_hbm, vu_hbm, vd_hbm,
    st, mo, vo, own, par, in_r, in_l, h_hbm,
    a_v, at_v, dy_v, wg_v, wu_v, wd_v, actt_v, dg_v, du_v, da_v, stage,
    t_own, t_par, t_in, t_out, f_own, f_par, f_r, f_l, f_m, f_v, f_w, n_w, n_m, n_v,
    w_sem, big_sem, h_sem, stage_sem, par_sem, t_sem, out_sem, rs_sem, f_sem, n_sem, ag_sem, fwd_sem, d_send, d_recv,
):
    me = lax.axis_index("dp")
    z, core = lax.div(me, 2), lax.rem(me, 2)
    partner = me + 1 - 2 * core
    ends = (3 - z, z)
    behind = (z, 3 - z)
    ahead = (me + 2, me - 2)
    incoming = (in_r, in_l)
    copy = pltpu.make_async_copy

    def remote(src, dst, send, recv, to):
        return pltpu.make_async_remote_copy(
            src_ref=src, dst_ref=dst, send_sem=send, recv_sem=recv, device_id={"dp": to}, device_id_type=MESH
        )

    barrier = pltpu.get_barrier_semaphore()
    pl.semaphore_signal(barrier, inc=1, device_id={"dp": partner}, device_id_type=MESH)
    for way in WAYS:

        @pl.when(ends[way] >= 1)
        def _():
            pl.semaphore_signal(barrier, inc=1, device_id={"dp": ahead[way]}, device_id_type=MESH)

    def strips(src, dst, sem, row, rows, layer, tile):
        for i in range(OWNERS):
            copy(
                src.at[layer, pl.ds(row, rows), pl.ds(pl.multiple_of(512 * i + W * tile, W), W)],
                dst.at[:, pl.ds(W * i, W)],
                sem,
            ).start()

    def weights_in(layer, tile, slot=0):
        strips(wg_hbm, wg_v.at[slot], w_sem.at[slot, 0], 0, D, layer, tile)
        strips(wu_hbm, wu_v.at[slot], w_sem.at[slot, 1], 0, D, layer, tile)

    def down_in(layer, tile, slot=0):
        for i in range(OWNERS):
            copy(
                wd_hbm.at[layer, pl.ds(pl.multiple_of(512 * i + W * tile, W), W), :],
                wd_v.at[slot, pl.ds(W * i, W), :],
                w_sem.at[slot, 2],
            ).start()

    def weights_wait(slot=0):
        for number, w in enumerate((wg_v, wu_v, wd_v)):
            copy(w.at[slot], w.at[slot], w_sem.at[slot, number]).wait()


    def at_block(i):
        return pl.ds(pl.multiple_of(i * W, W), W)

    def live(u):
        return (u >= 0) & (u < UNITS)

    def sends(way, hop, u):
        return live(u) & (behind[way] <= hop - 1) & (ends[way] >= 1)

    def sum_begin(u, hop):
        for way in WAYS:
            block = z + 4 - hop if way == 0 else z + hop - 4

            @pl.when(sends(way, hop, u))
            def _():
                copy(own.at[u, block], t_own.at[way], t_sem.at[way, 0]).start()
                copy(par.at[u, block], t_par.at[way], t_sem.at[way, 1]).start()

            if hop > 1:

                @pl.when(sends(way, hop, u) & (behind[way] >= 1))
                def _():
                    landed = incoming[way].at[u, hop - 2]
                    remote(landed, landed, out_sem.at[way, hop - 1], rs_sem.at[way, u, hop - 2], partner).wait_recv()
                    copy(landed, t_in.at[way], t_sem.at[way, 2]).start()

    def sum_out(way, hop, u):
        return remote(
            t_out.at[way, hop - 1],
            incoming[way].at[u, hop - 1],
            out_sem.at[way, hop - 1],
            rs_sem.at[way, u, hop - 1],
            ahead[way],
        )

    def sum_finish(u, hop):
        for way in WAYS:

            @pl.when(sends(way, hop, u) & (u >= 1))
            def _():
                sum_out(way, hop, u - 1).wait_send()

            @pl.when(sends(way, hop, u))
            def _():
                copy(own.at[u, 0], t_own.at[way], t_sem.at[way, 0]).wait()
                copy(par.at[u, 0], t_par.at[way], t_sem.at[way, 1]).wait()

                @pl.when(behind[way] == 0)
                def _():
                    t_out[way, hop - 1] = (t_own[way].astype(F32) + t_par[way].astype(F32)).astype(BF16)

                if hop > 1:

                    @pl.when(behind[way] >= 1)
                    def _():
                        copy(own.at[u, 0], t_in.at[way], t_sem.at[way, 2]).wait()
                        t_out[way, hop - 1] = (
                            t_own[way].astype(F32) + t_par[way].astype(F32) + t_in[way].astype(F32)
                        ).astype(BF16)

                sum_out(way, hop, u).start()

    def kind(u):
        tile = lax.div(u, 3)
        return lax.rem(u, 3), 1 - lax.div(tile, 4), lax.rem(tile, 4)

    def step_begin(u):
        @pl.when(live(u))
        def _():
            copy(own.at[u, z], f_own, f_sem.at[0]).start()
            copy(par.at[u, z], f_par, f_sem.at[1]).start()
            matrix, layer, tile = kind(u)

            @pl.when(matrix == 0)
            def _():
                copy(md_hbm.at[layer, at_block(tile), :], f_m, f_sem.at[4]).start()
                copy(vd_hbm.at[layer, at_block(tile), :], f_v, f_sem.at[5]).start()
                row = pl.ds(pl.multiple_of(512 * me + W * tile, W), W)
                copy(wd_hbm.at[layer, row, :], f_w, f_sem.at[6]).start()

            for number, (m, v, w) in enumerate(((mg_hbm, vg_hbm, wg_hbm), (mu_hbm, vu_hbm, wu_hbm))):

                @pl.when(matrix == number + 1)
                def _():
                    strips(m, f_m, f_sem.at[4], 0, W, layer, tile)
                    strips(v, f_v, f_sem.at[5], 0, W, layer, tile)
                    strips(w, f_w, f_sem.at[6], pl.multiple_of(W * me, W), W, layer, tile)

            for way, f_in in enumerate((f_r, f_l)):

                @pl.when(behind[way] >= 1)
                def _():
                    landed = incoming[way].at[u, 2]
                    remote(landed, landed, out_sem.at[way, 2], rs_sem.at[way, u, 2], partner).wait_recv()
                    copy(landed, f_in, f_sem.at[2 + way]).start()

    def results(u):
        slot = lax.rem(u + 2, 2)
        here = st.at[u, me]
        for way in WAYS:
            yield ends[way] >= 1, remote(n_w.at[slot], here, n_sem.at[slot, way], ag_sem.at[way, u, 0], ahead[way])
        yield None, remote(n_w.at[slot], here, n_sem.at[slot, 2], d_recv.at[u], partner)
        yield None, copy(n_w.at[slot], here, n_sem.at[slot, 3])
        yield None, copy(n_m.at[slot], mo.at[u], n_sem.at[slot, 4])
        yield None, copy(n_v.at[slot], vo.at[u], n_sem.at[slot, 5])

    def results_start(u):
        for condition, c in results(u):
            if condition is None:
                c.start()
            else:
                pl.when(condition)(c.start)

    def results_wait(u):
        for number, (condition, c) in enumerate(results(u)):
            wait = c.wait_send if number < 3 else c.wait
            if condition is None:
                wait()
            else:
                pl.when(condition)(wait)

    def step_finish(u):
        @pl.when(live(u) & (u >= 2))
        def _():
            results_wait(u - 2)

        @pl.when(live(u))
        def _():
            slot = lax.rem(u + 2, 2)
            copy(own.at[u, 0], f_own, f_sem.at[0]).wait()
            copy(par.at[u, 0], f_par, f_sem.at[1]).wait()
            copy(mo.at[u], f_m, f_sem.at[4]).wait()
            copy(vo.at[u], f_v, f_sem.at[5]).wait()
            copy(own.at[u, 0], f_w, f_sem.at[6]).wait()
            for way, f_in in enumerate((f_r, f_l)):

                @pl.when(behind[way] >= 1)
                def _():
                    copy(own.at[u, 0], f_in, f_sem.at[2 + way]).wait()

            def update(rows, incoming_sum):
                g = f_own[rows, :].astype(F32) + f_par[rows, :].astype(F32) + incoming_sum
                g = g.astype(BF16).astype(F32)
                m = 0.9 * f_m[rows, :] + 0.1 * g
                v = 0.95 * f_v[rows, :] + 0.05 * g * g
                w = f_w[rows, :].astype(F32)
                n_m[slot, rows, :] = m
                n_v[slot, rows, :] = v
                n_w[slot, rows, :] = (w - 0.02 * (m * lax.rsqrt(v + 1e-8) + 0.1 * w)).astype(BF16)

            def updates(*incoming_sums):
                @pl.loop(0, W // 32)
                def _(r):
                    rows = pl.ds(pl.multiple_of(r * 32, 32), 32)
                    update(rows, sum(one[rows, :].astype(F32) for one in incoming_sums))

            pl.when(z == 0)(functools.partial(updates, f_l))
            pl.when(z == CHIPS - 1)(functools.partial(updates, f_r))
            pl.when((z > 0) & (z < CHIPS - 1))(functools.partial(updates, f_r, f_l))
            results_start(u)

    def gathered(way, hop, u):
        return st.at[u, me - 2 * (hop - 1) if way == 0 else me + 2 * (hop - 1)]

    def pass_on(way, hop, u):
        block = gathered(way, hop, u)
        return remote(block, block, fwd_sem.at[way, hop - 2], ag_sem.at[way, u, hop - 1], ahead[way])

    def across(way, hop, u):
        block = gathered(way, hop, u)
        return remote(block, block, d_send.at[way, hop - 2], d_recv.at[u], partner)

    def gather(u, hop):
        for way in WAYS:

            @pl.when(live(u) & (behind[way] >= hop - 1))
            def _():
                block = gathered(way, hop, u)
                remote(block, block, d_send.at[way, hop - 2], ag_sem.at[way, u, hop - 2], partner).wait_recv()
                if hop < 4:

                    @pl.when((ends[way] >= 1) & (u >= 1))
                    def _():
                        pass_on(way, hop, u - 1).wait_send()

                    @pl.when(ends[way] >= 1)
                    def _():
                        pass_on(way, hop, u).start()

                @pl.when(u >= 1)
                def _():
                    across(way, hop, u - 1).wait_send()

                across(way, hop, u).start()

    def links(n):
        j, phase = lax.div(n, 8), lax.rem(n, 8)

        @pl.when(phase == 0)
        def _():
            @pl.when(live(j))
            def _():
                remote(own.at[j], par.at[j], stage_sem.at[0, 1], par_sem.at[j], partner).wait_recv()

            sum_begin(j, 1)
            gather(j - 3, 2)

        @pl.when(phase == 1)
        def _():
            sum_finish(j, 1)

        @pl.when(phase == 2)
        def _():
            step_begin(j - 2)

        @pl.when(phase == 3)
        def _():
            step_finish(j - 2)

        @pl.when(phase == 4)
        def _():
            sum_begin(j - 1, 3)
            gather(j - 4, 4)

        @pl.when(phase == 5)
        def _():
            sum_finish(j - 1, 3)

        @pl.when(phase == 6)
        def _():
            sum_begin(j, 2)
            gather(j - 3, 3)

        @pl.when(phase == 7)
        def _():
            sum_finish(j, 2)


    def stage_copies(n):
        slot, u, q = lax.rem(n, 2), lax.div(n, 4), lax.rem(n, 4)
        stay = copy(stage.at[slot, at_block(core), :], own.at[u, q], stage_sem.at[slot, 0])
        go = remote(stage.at[slot, at_block(1 - core), :], par.at[u, q], stage_sem.at[slot, 1], par_sem.at[u], partner)
        return stay, go

    def stage_wait(n):
        stay, go = stage_copies(n)
        stay.wait()
        go.wait_send()

    def gradient(tile, matrix, q, left, right):
        n = (3 * tile + matrix) * 4 + q
        rows = pl.ds(pl.multiple_of(q * 256, 256), 256)
        stage[lax.rem(n, 2)] = dot(left[rows, :], right[...]).astype(BF16)
        for c in stage_copies(n):
            c.start()

    def chunk(k, rows=512):
        return pl.ds(pl.multiple_of(k * rows, rows), rows)

    half = T // 2

    def x_in(c):
        return copy(x_hbm.at[chunk(c, half), :], du_v.at[chunk(c, half), :], h_sem.at[c])

    def h_out(c):
        return copy(du_v.at[chunk(c, half), :], h_hbm.at[chunk(c, half), :], h_sem.at[c])

    for c in (0, 1):
        x_in(c).start()
    weights_in(0, 0)
    down_in(0, 0)
    copy(dy_hbm, dy_v, big_sem.at[1]).start()

    def forward(t, carry):
        tile, c = lax.div(t, 2), lax.rem(t, 2)
        slot = lax.rem(tile, 2)

        @pl.when(tile == 0)
        def _():
            x_in(c).wait()

            @pl.loop(0, 8)
            def _(r):
                rows = pl.ds(pl.multiple_of(c * half + r * W, W), W)
                a_v[rows, :] = normed(du_v[rows, :].astype(F32))

        @pl.when(c == 0)
        def _():
            weights_wait(slot)
            ahead = lax.div(tile + 1, 4), lax.rem(tile + 1, 4), 1 - slot
            weights_in(*ahead)
            down_in(*ahead)

        rows = chunk(c, half)
        for n in range(4):
            cols = pl.ds(256 * n, 256)
            a = a_v[rows, :]
            gate = dot(a, wg_v[slot, :, cols])
            up = dot(a, wu_v[slot, :, cols])
            dg_v[rows, cols] = (gate * jax.nn.sigmoid(gate) * up).astype(BF16)
        more = dot(dg_v[rows, :], wd_v[slot])

        @pl.when(tile == 0)
        def _():
            da_v[rows, :] = more

        @pl.when(tile > 0)
        def _():
            da_v[rows, :] += more

        @pl.when(tile == 3)
        def _():
            @pl.loop(0, 8)
            def _(r):
                rows = pl.ds(pl.multiple_of(c * half + r * W, W), W)
                h = (du_v[rows, :].astype(F32) + da_v[rows, :].astype(BF16).astype(F32)).astype(BF16)
                du_v[rows, :] = h
                a_v[rows, :] = normed(h.astype(F32))

            h_out(c).start()

        return carry

    lax.fori_loop(0, 8, forward, 0)

    def hidden(rows, cols):
        a = a_v[rows, :]
        gate = dot(a, wg_v[0, :, cols])
        up = dot(a, wu_v[0, :, cols])
        back = dot(dy_v[rows, :], wd_v[0, cols, :], ALONG).astype(BF16).astype(F32)
        sig = jax.nn.sigmoid(gate)
        silu = gate * sig
        actt_v[cols, rows] = (silu * up).astype(BF16).T
        du_v[rows, cols] = (back * silu).astype(BF16)
        dg_v[rows, cols] = (back * up * (sig * (1.0 + gate * (1.0 - sig)))).astype(BF16)

    weights_wait()
    copy(dy_hbm, dy_v, big_sem.at[1]).wait()

    def first(c, carry):
        h_out(c).wait()
        for n in range(4):
            hidden(chunk(c, half), pl.ds(256 * n, 256))
        return carry

    lax.fori_loop(0, 2, first, 0)
    pl.semaphore_wait(barrier, 1 + (z > 0).astype(jnp.int32) + (z < 3).astype(jnp.int32))

    def body(t, carry):
        tile, k = lax.div(t, STEPS), lax.rem(t, STEPS)
        top = tile < 4

        pl.when(k == 0)(weights_wait)

        @pl.when((k == 0) & (tile == 4))
        def _():
            copy(x_hbm, a_v, big_sem.at[0]).wait()

            @pl.loop(0, 8)
            def _(c):
                a_v[chunk(c, 256), :] = normed(a_v[chunk(c, 256), :].astype(F32))

        @pl.when(k < 8)
        def _():
            hidden(chunk(lax.div(k, 2)), chunk(lax.rem(k, 2)))

        @pl.when((k == 8) & (tile < 7))
        def _():
            down_in(1 - lax.div(tile + 1, 4), lax.rem(tile + 1, 4))

        @pl.when((k == 8) & (tile == 3))
        def _():
            copy(h_hbm, a_v, big_sem.at[0]).start()

        @pl.when((k >= 8) & (k < 12))
        def _():
            gradient(tile, 0, k - 8, actt_v, dy_v)

        @pl.when((k >= 12) & (k < 16) & (lax.rem(tile, 4) == 0))
        def _():
            rows = chunk(k - 12)
            at_v[:, rows] = a_v[rows, :].T

        @pl.when((k >= 12) & (k < 16) & top)
        def _():
            rows = chunk(k - 12)
            more = dot(dg_v[rows, :], wg_v[0], ALONG) + dot(du_v[rows, :], wu_v[0], ALONG)

            @pl.when(tile == 0)
            def _():
                da_v[rows, :] = more

            @pl.when(tile > 0)
            def _():
                da_v[rows, :] += more

        @pl.when((k == 12) & (tile == 3))
        def _():
            copy(h_hbm, a_v, big_sem.at[0]).wait()

        @pl.when((k >= 12) & (k < 16) & (tile == 3))
        def _():
            @pl.loop(0, 4)
            def _(r):
                rows = pl.ds(pl.multiple_of((k - 12) * 512 + r * 128, 128), 128)
                wide = a_v[rows, :].astype(F32)
                da = da_v[rows, :].astype(BF16).astype(F32)
                scale = lax.rsqrt(jnp.mean(wide * wide, -1, keepdims=True) + 1e-6)
                along = jnp.sum(da * wide, -1, keepdims=True) * (scale * scale * scale) * (1.0 / D)
                dh = (da * scale - wide * along).astype(BF16)
                dy_v[rows, :] = (dy_v[rows, :].astype(F32) + dh.astype(F32)).astype(BF16)

        @pl.when((k == 16) & (tile < 7))
        def _():
            weights_in(1 - lax.div(tile + 1, 4), lax.rem(tile + 1, 4))

        @pl.when((k == 16) & (tile == 3))
        def _():
            copy(x_hbm, a_v, big_sem.at[0]).start()

        @pl.when((k >= 16) & (k < 20))
        def _():
            gradient(tile, 1, k - 16, at_v, dg_v)

        @pl.when(k >= 20)
        def _():
            gradient(tile, 2, k - 20, at_v, du_v)

        @pl.when((k >= 9) & (k < 13))
        def _():
            stage_wait(12 * tile + k - 9)

        @pl.when(k >= 17)
        def _():
            stage_wait(12 * tile + 4 + k - 17)

        @pl.when((k == 0) & (tile > 0))
        def _():
            stage_wait(12 * tile - 1)

        @pl.when(t >= 12)
        def _():
            links(t - 12)

        return carry

    lax.fori_loop(8, TILES * STEPS, body, 0)
    stage_wait(4 * UNITS - 1)

    def rest(n, carry):
        links(n)
        return carry

    lax.fori_loop(TILES * STEPS - 12, 27 * 8 + 5, rest, 0)

    last = UNITS - 1
    for way in WAYS:
        for hop in (1, 2, 3):
            pl.when(sends(way, hop, last))(sum_out(way, hop, last).wait_send)
        for hop in (2, 3, 4):

            @pl.when(behind[way] >= hop - 1)
            def _():
                if hop < 4:
                    pl.when(ends[way] >= 1)(pass_on(way, hop, last).wait_send)
                across(way, hop, last).wait_send()

    results_wait(last - 1)
    results_wait(last)

    def arrived(u, carry):
        remote(own.at[u], par.at[u], d_send.at[0, 0], d_recv.at[u], partner).wait_recv()
        return carry

    lax.fori_loop(0, UNITS, arrived, 0)


def run_main(*args):
    like = jax.ShapeDtypeStruct
    any_spec = pl.BlockSpec(memory_space=pl.ANY)
    block = (W, D)
    outs = [(OWNERS, BF16), (1, F32), (1, F32), (CHIPS, BF16), (CHIPS, BF16), (3, BF16), (3, BF16)]
    wide, deep, blocks, pair = (T, D), (D, T), (2, *block), (2, 3)
    scratch = [(wide, BF16), (deep, BF16), (wide, BF16), *[((2, D, TILE), BF16)] * 3, (deep, BF16), *[(wide, BF16)] * 2, (wide, F32)]
    scratch += [((2, 256, D), BF16), *[(blocks, BF16)] * 3, ((2, 3, *block), BF16), *[(block, BF16)] * 4, *[(block, F32)] * 2]
    scratch += [(block, BF16), (blocks, BF16), (blocks, F32), (blocks, F32)]
    sems = [pair, (2,), (2,), (2, 2), (UNITS,), pair, pair, (2, UNITS, 3), (7,), (2, 6), (2, UNITS, 3), (2, 2), pair, (UNITS,)]
    return pl.pallas_call(
        main,
        name="main",
        in_specs=[any_spec] * len(args),
        out_specs=[any_spec] * (len(outs) + 1),
        out_shape=[*[like((UNITS, n, *block) if n > 1 else (UNITS, *block), t) for n, t in outs], like(wide, BF16)],
        scratch_shapes=[*[pltpu.VMEM(*one) for one in scratch], *[pltpu.SemaphoreType.DMA(one) for one in sems]],
        compiler_params=pltpu.CompilerParams(collective_id=0, has_side_effects=True, vmem_limit_bytes=VMEM_LIMIT),
        cost_estimate=pl.CostEstimate(flops=34 * T * D * FF, bytes_accessed=600 << 20, transcendentals=3 * T * FF),
    )(*args)


GROUP = 4
PARTS = OWNERS // GROUP


def lay_out(st_ref, m_ref, v_ref, *outs):
    matrix = lax.div(pl.program_id(0), 2 * PARTS)
    moment = W // PARTS

    for number in range(3):
        w_out, m_out, v_out = outs[number::3]

        @pl.when(matrix == number)
        def _():
            for tile in range(4):
                for src, dst in ((st_ref, w_out), (m_ref, m_out), (v_ref, v_out)):
                    rows = W if src is st_ref else moment
                    for o in range(GROUP if src is st_ref else 1):
                        block = src.at[0, tile, 0, o] if src is st_ref else src.at[0, tile, 0]
                        if number == 2:
                            dst[0, o, tile] = block[...]
                        else:
                            for i in range(OWNERS):
                                dst[0, pl.ds(rows * o, rows), pl.ds(512 * i + W * tile, W)] = block[:, pl.ds(W * i, W)]


def run_lay_out(st, mo, vo):
    per = 2 * PARTS
    moment = W // PARTS

    def at(number, s):
        own = jnp.clip(s - number * per, 0, per - 1)
        return lax.div(own, PARTS), lax.rem(own, PARTS)

    def source(s):
        number, own = lax.div(s, per), lax.rem(s, per)
        return 1 - lax.div(own, PARTS), lax.rem(number + 1, 3), lax.rem(own, PARTS)

    def into(s):
        layer, matrix, part = source(s)
        return layer, 0, matrix, part, 0, 0

    def moments_into(s):
        layer, matrix, part = source(s)
        return layer, 0, matrix, part, 0

    like = jax.ShapeDtypeStruct
    specs, shapes = [], []
    for rows, kind in ((GROUP, BF16), (1, F32), (1, F32)):
        for number in range(3):
            height = W if kind == BF16 else moment
            if number == 2:
                block, whole = (1, rows, 4, height, D), (2, OWNERS if kind == BF16 else 1, 4, W, D)
                where = (lambda s: (*at(2, s), 0, 0, 0)) if kind == BF16 else (lambda s: (at(2, s)[0], 0, 0, at(2, s)[1], 0))
            else:
                block, whole = (1, rows * height, FF), (2, D if kind == BF16 else W, FF)
                where = functools.partial(lambda number, s: (*at(number, s), 0), number)
            specs.append(pl.BlockSpec(block, where))
            shapes.append(like(whole, kind))
    moments = pl.BlockSpec((1, 4, 1, moment, D), moments_into)
    out = pl.pallas_call(
        lay_out,
        name="lay_out",
        grid=(3 * per,),
        in_specs=[pl.BlockSpec((1, 4, 1, GROUP, W, D), into), moments, moments],
        out_specs=specs,
        out_shape=shapes,
        compiler_params=pltpu.CompilerParams(dimension_semantics=("arbitrary",), vmem_limit_bytes=VMEM_LIMIT),
    )(st, mo, vo)
    return [t.reshape(2, -1, t.shape[-1]) for t in out]


def solution(mesh):
    def step(x, dy, w_gate, w_up, w_down, m_gate, m_up, m_down, v_gate, v_up, v_down):
        x, dy = x[0], dy[0]
        st, mo, vo, *_ = run_main(x, dy, w_gate, w_up, w_down, m_gate, m_up, m_down, v_gate, v_up, v_down)
        st = st.reshape(2, 4, 3, OWNERS, W, D)
        mo, vo = (t.reshape(2, 4, 3, W, D) for t in (mo, vo))
        return tuple(run_lay_out(st, mo, vo))

    rows = P(None, "dp", None)
    sequences = P(("rep", "dp"), None, None)
    return jax.shard_map(
        step,
        mesh=mesh,
        in_specs=(sequences, sequences, *[P(None, None, None)] * 3, *[rows] * 6),
        out_specs=(*[P("rep", None, None)] * 3, *[P("rep", "dp", None)] * 6),
        check_vma=False,
    )
```

time: 1720 us -> 725 us (0.42)
  waiting for transfers between devices: 1150 us -> 0 us
  Pallas kernels: 0 us -> 724 us
  matrix products: 397 us -> 0 us
  other arithmetic: 100 us -> 0 us
  local copies, waits for them, and re-layouts: 51 us -> 0 us
    pallas_call x0 -> x2, Pallas kernels: none -> 724 us  [the longest x1 676 us: run_main(): pl.pallas_call(main, name='main', in_specs=[any_spec] * len(args), out_sp...]
    unnamed x15 -> x0, waiting for transfers between devices: 701 us -> none
    reshape x3 -> x0, waiting for transfers between devices: 446 us -> none  [step(): t.reshape(-1, *t.shape[2:])]
    dot_general x15 -> x0, matrix products: 397 us -> none  [the longest x5 136 us: layer(): gate = jnp.dot(a, w['w_gate'], preferred_element_type=jnp.float32)]
    unnamed x4 -> x0, other arithmetic: 63.6 us -> none
    unnamed x39 -> x0, local copies, waits for them, and re-layouts: 50.4 us -> none
    reshape x3 -> x0, other arithmetic: 23 us -> none  [step(): t.reshape(-1, *t.shape[2:])]
  transfers between devices with their start and end apart: 9 -> 0, of which waited for: 8 -> 0; matrix products, arithmetic and copies ran while one was open for 19% -> 0% of each run, Pallas kernels for 0% -> 0%
where the time goes in v1:
time: 725 us
  Pallas kernels  724 us (100%)
    pallas_call x1, Pallas kernels, run_main(): pl.pallas_call(main, name='main', in_specs=[any_spec] * len(args), out_sp...  676 us
    pallas_call x1, Pallas kernels, run_lay_out(): pl.pallas_call(lay_out, name='lay_out', grid=(3 * per,), in_specs=[pl.Blo...  48.4 us

profile of v1, /device:TPU:0, one launch (start us, length us, event | category | flops | bytes accessed | tf_op | source)
XLA Modules:
  0.0 724.8 jit_solution(12935166238834783177)
XLA Ops:
  0.6 675.7 %main.1 = (bf16[24,8,128,1024]{3,2,1,0:T(8,128)(2,1)}, f32[24,128,1024]{2,1,0:T(8,128)}, f32[24,128,1024]{2,1,0:T(8,128)}, bf16[24,4,128,1024]{3,2,1,0:T(8,128)(...) custom-call(bf16[2048,1024]{1,0:T(8,128)(2,1)} %bitcast.12, ...), custom_call_target="tpu_custom_call" | custom-call | flops 292057776128 | bytes 629145600 | tf_op jit(solution)/shard_map/main/pallas_call | solution.py:574
  676.4 48.4 %lay_out.1 = (bf16[2,1024,4096]{2,1,0:T(8,128)(2,1)}, bf16[2,1024,4096]{2,1,0:T(8,128)(2,1)}, bf16[2,8,4,128,1024]{4,3,2,1,0:T(8,128)(2,1)}, f32[2,128,4096]{2,1...) custom-call(bf16[2,4,3,8,128,1024]{5,4,3,2,1,0:T(8,128)(2,1)} %bitca, ...), custom_call_target="tpu_custom_call" | custom-call | tf_op jit(solution)/shard_map/lay_out/pallas_call | solution.py:645

commit v2 on v1

v2 whole, which is shorter than its diff:
```python
import functools

import jax
import jax.numpy as jnp
from jax import lax
from jax.experimental import pallas as pl
from jax.experimental.pallas import tpu as pltpu
from jax.sharding import PartitionSpec as P

MESH = pl.DeviceIdType.MESH
T, D, FF = 2048, 1024, 4096
CHIPS = 4
OWNERS = 8
W = 128
TILE = 1024
UNITS = 24
STEPS = 24
TILES = 8
VMEM_LIMIT = 63 << 20
WAYS = (0, 1)
ALONG = ((1,), (1,))
F32, BF16 = jnp.float32, jnp.bfloat16
SUMS = ((10, 16, 20, 12), (13, 21, 24, 18), (19, 26, 32, 22))
STEP = (23, 35, 38, 29)
GATHERS = ((30, 43, 45, 36), (39, 48, 50, 41), (50, 55, 58, 48))
LAST = GATHERS[2][3] + 8 * (UNITS - 1)


def normed(wide):
    return (wide * lax.rsqrt(jnp.mean(wide * wide, -1, keepdims=True) + 1e-6)).astype(BF16)


def dot(a, b, dims=((1,), (0,))):
    return lax.dot_general(a, b, (dims, ((), ())), preferred_element_type=F32)


def main(
    x_hbm, dy_hbm, wg_hbm, wu_hbm, wd_hbm, mg_hbm, mu_hbm, md_hbm, vg_hbm, vu_hbm, vd_hbm,
    st, mo, vo, own, par, in_r, in_l,
    a_v, h_v, dy_v, wg_v, wu_v, wd_v, actt_v, dg_v, du_v, da_v, stage,
    t_own, t_par, t_in, t_out, f_own, f_par, f_r, f_l, f_m, f_v, f_w, n_w, n_m, n_v,
    w_sem, big_sem, x_sem, stage_sem, par_sem, t_sem, out_sem, rs_sem, f_sem, n_sem, ag_sem, fwd_sem, d_send, d_recv,
):
    me = lax.axis_index("dp")
    z, core = lax.div(me, 2), lax.rem(me, 2)
    partner = me + 1 - 2 * core
    ends = (3 - z, z)
    behind = (z, 3 - z)
    ahead = (me + 2, me - 2)
    incoming = (in_r, in_l)
    copy = pltpu.make_async_copy

    def remote(src, dst, send, recv, to):
        return pltpu.make_async_remote_copy(
            src_ref=src, dst_ref=dst, send_sem=send, recv_sem=recv, device_id={"dp": to}, device_id_type=MESH
        )

    barrier = pltpu.get_barrier_semaphore()
    pl.semaphore_signal(barrier, inc=1, device_id={"dp": partner}, device_id_type=MESH)
    for way in WAYS:

        @pl.when(ends[way] >= 1)
        def _():
            pl.semaphore_signal(barrier, inc=1, device_id={"dp": ahead[way]}, device_id_type=MESH)

    def strips(src, dst, sem, row, rows, layer, tile):
        for i in range(OWNERS):
            copy(
                src.at[layer, pl.ds(row, rows), pl.ds(pl.multiple_of(512 * i + W * tile, W), W)],
                dst.at[:, pl.ds(W * i, W)],
                sem,
            ).start()

    def weights_in(layer, tile, slot):
        strips(wg_hbm, wg_v.at[slot], w_sem.at[slot, 0], 0, D, layer, tile)
        strips(wu_hbm, wu_v.at[slot], w_sem.at[slot, 1], 0, D, layer, tile)
        for i in range(OWNERS):
            copy(
                wd_hbm.at[layer, pl.ds(pl.multiple_of(512 * i + W * tile, W), W), :],
                wd_v.at[slot, pl.ds(W * i, W), :],
                w_sem.at[slot, 2],
            ).start()

    def weights_wait(slot):
        for number, w in enumerate((wg_v, wu_v, wd_v)):
            copy(w.at[slot], w.at[slot], w_sem.at[slot, number]).wait()


    def at_block(i):
        return pl.ds(pl.multiple_of(i * W, W), W)

    def live(u):
        return (u >= 0) & (u < UNITS)

    def sends(way, hop):
        return (behind[way] <= hop - 1) & (ends[way] >= 1)

    def sum_begin(u, hop):
        def brought(blocks, sem):
            some = pl.ds(0, blocks)
            remote(own.at[0, some], par.at[0, some], stage_sem.at[0, 1], par_sem.at[sem], partner).wait_recv()

        if hop == 1:
            pl.when(u > 0)(functools.partial(brought, CHIPS, u))
        if hop < 3:
            pl.when(u == 0)(functools.partial(brought, 2, UNITS if hop == 1 else 0))
        for way in WAYS:
            block = z + 4 - hop if way == 0 else z + hop - 4

            @pl.when(sends(way, hop))
            def _():
                copy(own.at[u, block], t_own.at[way], t_sem.at[way, 0]).start()
                copy(par.at[u, block], t_par.at[way], t_sem.at[way, 1]).start()

            if hop > 1:

                @pl.when(sends(way, hop) & (behind[way] >= 1))
                def _():
                    landed = incoming[way].at[u, hop - 2]
                    remote(landed, landed, out_sem.at[way, hop - 1], rs_sem.at[way, u, hop - 2], partner).wait_recv()
                    copy(landed, t_in.at[way], t_sem.at[way, 2]).start()

    def sum_out(way, hop, u):
        return remote(
            t_out.at[way, hop - 1],
            incoming[way].at[u, hop - 1],
            out_sem.at[way, hop - 1],
            rs_sem.at[way, u, hop - 1],
            ahead[way],
        )

    def sum_finish(u, hop):
        for way in WAYS:

            @pl.when(sends(way, hop) & (u >= 1))
            def _():
                sum_out(way, hop, u - 1).wait_send()

            @pl.when(sends(way, hop))
            def _():
                copy(own.at[u, 0], t_own.at[way], t_sem.at[way, 0]).wait()
                copy(par.at[u, 0], t_par.at[way], t_sem.at[way, 1]).wait()

                @pl.when(behind[way] == 0)
                def _():
                    t_out[way, hop - 1] = (t_own[way].astype(F32) + t_par[way].astype(F32)).astype(BF16)

                if hop > 1:

                    @pl.when(behind[way] >= 1)
                    def _():
                        copy(own.at[u, 0], t_in.at[way], t_sem.at[way, 2]).wait()
                        t_out[way, hop - 1] = (
                            t_own[way].astype(F32) + t_par[way].astype(F32) + t_in[way].astype(F32)
                        ).astype(BF16)

                sum_out(way, hop, u).start()

    def kind(u):
        tile = lax.div(u, 3)
        return lax.rem(u, 3), 1 - lax.div(tile, 4), lax.rem(tile, 4)

    def step_begin(u):
        copy(own.at[u, z], f_own, f_sem.at[0]).start()
        copy(par.at[u, z], f_par, f_sem.at[1]).start()
        matrix, layer, tile = kind(u)

        @pl.when(matrix == 0)
        def _():
            copy(md_hbm.at[layer, at_block(tile), :], f_m, f_sem.at[4]).start()
            copy(vd_hbm.at[layer, at_block(tile), :], f_v, f_sem.at[5]).start()
            row = pl.ds(pl.multiple_of(512 * me + W * tile, W), W)
            copy(wd_hbm.at[layer, row, :], f_w, f_sem.at[6]).start()

        for number, (m, v, w) in enumerate(((mg_hbm, vg_hbm, wg_hbm), (mu_hbm, vu_hbm, wu_hbm))):

            @pl.when(matrix == number + 1)
            def _():
                strips(m, f_m, f_sem.at[4], 0, W, layer, tile)
                strips(v, f_v, f_sem.at[5], 0, W, layer, tile)
                strips(w, f_w, f_sem.at[6], pl.multiple_of(W * me, W), W, layer, tile)

        for way, f_in in enumerate((f_r, f_l)):

            @pl.when(behind[way] >= 1)
            def _():
                landed = incoming[way].at[u, 2]
                remote(landed, landed, out_sem.at[way, 2], rs_sem.at[way, u, 2], partner).wait_recv()
                copy(landed, f_in, f_sem.at[2 + way]).start()

    def results(u):
        slot = u & 1
        here = st.at[u, me]
        for way in WAYS:
            yield ends[way] >= 1, remote(n_w.at[slot], here, n_sem.at[slot, way], ag_sem.at[way, u, 0], ahead[way])
        yield None, remote(n_w.at[slot], here, n_sem.at[slot, 2], d_recv.at[u], partner)
        yield None, copy(n_w.at[slot], here, n_sem.at[slot, 3])
        yield None, copy(n_m.at[slot], mo.at[u], n_sem.at[slot, 4])
        yield None, copy(n_v.at[slot], vo.at[u], n_sem.at[slot, 5])

    def results_start(u):
        for condition, c in results(u):
            if condition is None:
                c.start()
            else:
                pl.when(condition)(c.start)

    def results_wait(u):
        for number, (condition, c) in enumerate(results(u)):
            wait = c.wait_send if number < 3 else c.wait
            if condition is None:
                wait()
            else:
                pl.when(condition)(wait)

    def step_finish(u):
        @pl.when(u >= 2)
        def _():
            results_wait(u - 2)

        slot = u & 1
        copy(own.at[u, 0], f_own, f_sem.at[0]).wait()
        copy(par.at[u, 0], f_par, f_sem.at[1]).wait()
        copy(mo.at[u], f_m, f_sem.at[4]).wait()
        copy(vo.at[u], f_v, f_sem.at[5]).wait()
        copy(own.at[u, 0], f_w, f_sem.at[6]).wait()
        for way, f_in in enumerate((f_r, f_l)):

            @pl.when(behind[way] >= 1)
            def _():
                copy(own.at[u, 0], f_in, f_sem.at[2 + way]).wait()

        def update(rows, incoming_sum):
            g = f_own[rows, :].astype(F32) + f_par[rows, :].astype(F32) + incoming_sum
            g = g.astype(BF16).astype(F32)
            m = 0.9 * f_m[rows, :] + 0.1 * g
            v = 0.95 * f_v[rows, :] + 0.05 * g * g
            w = f_w[rows, :].astype(F32)
            n_m[slot, rows, :] = m
            n_v[slot, rows, :] = v
            n_w[slot, rows, :] = (w - 0.02 * (m * lax.rsqrt(v + 1e-8) + 0.1 * w)).astype(BF16)

        def updates(*incoming_sums):
            @pl.loop(0, W // 32)
            def _(r):
                rows = pl.ds(pl.multiple_of(r * 32, 32), 32)
                update(rows, sum(one[rows, :].astype(F32) for one in incoming_sums))

        pl.when(z == 0)(functools.partial(updates, f_l))
        pl.when(z == CHIPS - 1)(functools.partial(updates, f_r))
        pl.when((z > 0) & (z < CHIPS - 1))(functools.partial(updates, f_r, f_l))
        results_start(u)

    def gathered(way, hop, u):
        return st.at[u, me - 2 * (hop - 1) if way == 0 else me + 2 * (hop - 1)]

    def pass_on(way, hop, u):
        block = gathered(way, hop, u)
        return remote(block, block, fwd_sem.at[way, hop - 2], ag_sem.at[way, u, hop - 1], ahead[way])

    def across(way, hop, u):
        block = gathered(way, hop, u)
        return remote(block, block, d_send.at[way, hop - 2], d_recv.at[u], partner)

    def gather(u, hop):
        for way in WAYS:

            @pl.when(behind[way] >= hop - 1)
            def _():
                block = gathered(way, hop, u)
                remote(block, block, d_send.at[way, hop - 2], ag_sem.at[way, u, hop - 2], partner).wait_recv()
                if hop < 4:

                    @pl.when((ends[way] >= 1) & (u >= 1))
                    def _():
                        pass_on(way, hop, u - 1).wait_send()

                    @pl.when(ends[way] >= 1)
                    def _():
                        pass_on(way, hop, u).start()

                @pl.when(u >= 1)
                def _():
                    across(way, hop, u - 1).wait_send()

                across(way, hop, u).start()

    def turn(when, b, later, what, *args):
        late = when[3] + later
        u = jnp.where((b & 7 == late % 8) & (b >= late + 24), (b >> 3) - late // 8, -1)
        for early in range(3):
            u = jnp.where(b == when[early] + later, early, u)
        pl.when(live(u))(lambda: what(u, *args))

    def links(b):
        for hop in (1, 2, 3):
            turn(SUMS[hop - 1], b, 1, sum_finish, hop)
        turn(STEP, b, 1, step_finish)
        turn(SUMS[1], b, 0, sum_begin, 2)
        turn(GATHERS[2], b, 0, gather, 4)
        turn(SUMS[0], b, 0, sum_begin, 1)
        turn(SUMS[2], b, 0, sum_begin, 3)
        turn(GATHERS[1], b, 0, gather, 3)
        turn(GATHERS[0], b, 0, gather, 2)
        turn(STEP, b, 0, step_begin)


    def stage_copies(n):
        slot, u, q = n & 1, n >> 2, n & 3
        stay = copy(stage.at[slot, at_block(core), :], own.at[u, q], stage_sem.at[slot, 0])
        sem = jnp.where((n == 0) | (n == 3), UNITS, u)
        go = remote(stage.at[slot, at_block(1 - core), :], par.at[u, q], stage_sem.at[slot, 1], par_sem.at[sem], partner)
        return stay, go

    def stage_wait(n):
        stay, go = stage_copies(n)
        stay.wait()
        go.wait_send()

    def gradient(tile, matrix, q):
        n = (3 * tile + matrix) * 4 + q
        at = chunk(q, 256)
        if matrix == 0:
            g = dot(actt_v[at, :], dy_v[...])
        else:
            g = dot(a_v[:, at], (dg_v if matrix == 1 else du_v)[...], ((0,), (0,)))
        stage[n & 1] = g.astype(BF16)
        for c in stage_copies(n):
            c.start()

    def chunk(k, rows=512):
        return pl.ds(pl.multiple_of(k * rows, rows), rows)

    half = T // 2

    def x_in(c):
        return copy(x_hbm.at[chunk(c, half), :], du_v.at[chunk(c, half), :], x_sem.at[c])

    def plain_in(tile, slot):
        at = chunk(tile, TILE)
        copy(wg_hbm.at[0, :, at], wg_v.at[slot], w_sem.at[slot, 0]).start()
        copy(wu_hbm.at[0, :, at], wu_v.at[slot], w_sem.at[slot, 1]).start()
        copy(wd_hbm.at[0, at, :], wd_v.at[slot], w_sem.at[slot, 2]).start()

    x_in(0).start()
    plain_in(0, 0)
    x_in(1).start()
    da_v[...] = jnp.zeros_like(da_v)

    def forward(t, carry):
        tile, c = lax.div(t, 2), lax.rem(t, 2)
        slot = lax.rem(tile, 2)

        @pl.when(tile == 0)
        def _():
            x_in(c).wait()
            for r in WAYS:
                rows = chunk(2 * c + r)
                a_v[rows, :] = normed(du_v[rows, :].astype(F32))

        @pl.when(c == 0)
        def _():
            weights_wait(slot)
            pl.when(tile == 2)(copy(dy_hbm, dy_v, big_sem.at[1]).start)
            pl.when(tile < 3)(lambda: plain_in(tile + 1, 1 - slot))
            pl.when(tile == 3)(lambda: weights_in(1, 0, 0))

        rows = chunk(c, half)
        for n in range(4):
            cols = pl.ds(256 * n, 256)
            a = a_v[rows, :]
            gate = dot(a, wg_v[slot, :, cols])
            up = dot(a, wu_v[slot, :, cols])
            dg_v[rows, cols] = (gate * jax.nn.sigmoid(gate) * up).astype(BF16)
        da_v[rows, :] += dot(dg_v[rows, :], wd_v[slot])

        @pl.when(tile == 3)
        def _():
            for r in WAYS:
                rows = chunk(2 * c + r)
                h = (du_v[rows, :].astype(F32) + da_v[rows, :].astype(BF16).astype(F32)).astype(BF16)
                h_v[rows, :] = h
                a_v[rows, :] = normed(h.astype(F32))
                da_v[rows, :] = jnp.zeros((512, D), F32)

        return carry

    lax.fori_loop(0, 8, forward, 0)

    def hidden(rows, cols, slot):
        a = a_v[rows, :]
        gate = dot(a, wg_v[slot, :, cols])
        up = dot(a, wu_v[slot, :, cols])
        back = dot(dy_v[rows, :], wd_v[slot, cols, :], ALONG).astype(BF16).astype(F32)
        sig = jax.nn.sigmoid(gate)
        silu = gate * sig
        actt_v[cols, rows] = (silu * up).astype(BF16).T
        du_v[rows, cols] = (back * silu).astype(BF16)
        dg_v[rows, cols] = (back * up * (sig * (1.0 + gate * (1.0 - sig)))).astype(BF16)

    weights_wait(0)
    copy(dy_hbm, dy_v, big_sem.at[1]).wait()
    pl.semaphore_wait(barrier, 1 + (z > 0).astype(jnp.int32) + (z < 3).astype(jnp.int32))

    def first(p, carry):
        inner, c = lax.div(p, 2), lax.rem(p, 2)
        for i in WAYS:
            hidden(chunk(c, half), chunk(inner + i * (3 - 2 * inner), 256), 0)

        @pl.when(p == 2)
        def _():
            stage_wait(0)
            stage_wait(3)

        @pl.when(p >= 2)
        def _():
            links(p + 8)

        @pl.when(c == 1)
        def _():
            def one(i, carry):
                gradient(0, 0, 2 * inner + i * (3 - 4 * inner))
                return carry

            lax.fori_loop(0, 2, one, 0)

        return carry

    lax.fori_loop(0, 4, first, 0)
    stage_wait(2)

    def body(t, carry):
        tile, k = lax.div(t, STEPS), lax.rem(t, STEPS)
        slot = lax.rem(tile, 2)

        @pl.when(k == 0)
        def _():
            weights_wait(slot)

            @pl.when(tile == 4)
            def _():
                copy(x_hbm, a_v, big_sem.at[0]).wait()
                for c in range(4):
                    a_v[chunk(c), :] = normed(a_v[chunk(c), :].astype(F32))

        @pl.when(k < 8)
        def _():
            hidden(chunk(lax.div(k, 2)), chunk(lax.rem(k, 2)), slot)

        pl.when(((k == 8) & (tile < 7)) | (t == 12))(
            lambda: weights_in(1 - lax.div(tile + 1, 4), lax.rem(tile + 1, 4), 1 - slot)
        )

        for matrix in range(3):
            pl.when((k >= 8 + 4 * matrix) & (k < 12 + 4 * matrix))(
                functools.partial(gradient, tile, matrix, k - 8 - 4 * matrix)
            )

        pl.when((k == 20) & (tile == 3))(copy(x_hbm, a_v, big_sem.at[0]).start)

        @pl.when((k >= 20) & (tile < 4))
        def _():
            rows = chunk(k - 20)
            da_v[rows, :] += dot(dg_v[rows, :], wg_v[slot], ALONG) + dot(du_v[rows, :], wu_v[slot], ALONG)

        @pl.when((k >= 20) & (tile == 3))
        def _():
            @pl.loop(0, 4)
            def _(r):
                rows = pl.ds(pl.multiple_of((k - 20) * 512 + r * W, W), W)
                wide = h_v[rows, :].astype(F32)
                da = da_v[rows, :].astype(BF16).astype(F32)
                scale = lax.rsqrt(jnp.mean(wide * wide, -1, keepdims=True) + 1e-6)
                along = jnp.sum(da * wide, -1, keepdims=True) * (scale * scale * scale) * (1.0 / D)
                dh = (da * scale - wide * along).astype(BF16)
                dy_v[rows, :] = (dy_v[rows, :].astype(F32) + dh.astype(F32)).astype(BF16)

        @pl.when((k >= 9) & (k < 21))
        def _():
            stage_wait(jnp.where(t == 12, 1, 12 * tile + k - 9))

        links(t)
        return carry

    lax.fori_loop(12, TILES * STEPS, body, 0)

    def rest(b, carry):
        links(b)
        return carry

    lax.fori_loop(TILES * STEPS, LAST + 1, rest, 0)

    last = UNITS - 1
    for way in WAYS:
        for hop in (1, 2, 3):
            pl.when(sends(way, hop))(sum_out(way, hop, last).wait_send)
        for hop in (2, 3, 4):

            @pl.when(behind[way] >= hop - 1)
            def _():
                if hop < 4:
                    pl.when(ends[way] >= 1)(pass_on(way, hop, last).wait_send)
                across(way, hop, last).wait_send()

    results_wait(last - 1)
    results_wait(last)

    def arrived(u, carry):
        remote(own.at[u], par.at[u], d_send.at[0, 0], d_recv.at[u], partner).wait_recv()
        return carry

    lax.fori_loop(0, UNITS, arrived, 0)


def run_main(*args):
    like = jax.ShapeDtypeStruct
    any_spec = pl.BlockSpec(memory_space=pl.ANY)
    block = (W, D)
    outs = [(OWNERS, BF16), (1, F32), (1, F32), (CHIPS, BF16), (CHIPS, BF16), (3, BF16), (3, BF16)]
    wide, deep, blocks, pair = (T, D), (D, T), (2, *block), (2, 3)
    scratch = [*[(wide, BF16)] * 3, *[((2, D, TILE), BF16)] * 3, (deep, BF16), *[(wide, BF16)] * 2, (wide, F32)]
    scratch += [((2, 256, D), BF16), *[(blocks, BF16)] * 3, ((2, 3, *block), BF16), *[(block, BF16)] * 4, *[(block, F32)] * 2]
    scratch += [(block, BF16), (blocks, BF16), (blocks, F32), (blocks, F32)]
    sems = [pair, (2,), (2,), (2, 2), (UNITS + 1,), pair, pair, (2, UNITS, 3), (7,), (2, 6), (2, UNITS, 3), (2, 2), pair, (UNITS,)]
    return pl.pallas_call(
        main,
        name="main",
        in_specs=[any_spec] * len(args),
        out_specs=[any_spec] * len(outs),
        out_shape=[like((UNITS, n, *block) if n > 1 else (UNITS, *block), t) for n, t in outs],
        scratch_shapes=[*[pltpu.VMEM(*one) for one in scratch], *[pltpu.SemaphoreType.DMA(one) for one in sems]],
        compiler_params=pltpu.CompilerParams(collective_id=0, has_side_effects=True, vmem_limit_bytes=VMEM_LIMIT),
        cost_estimate=pl.CostEstimate(flops=34 * T * D * FF, bytes_accessed=600 << 20, transcendentals=3 * T * FF),
    )(*args)


GROUP = 4
PARTS = OWNERS // GROUP


def lay_out(st_ref, m_ref, v_ref, *outs):
    matrix = lax.div(pl.program_id(0), 2 * PARTS)
    moment = W // PARTS

    for number in range(3):
        w_out, m_out, v_out = outs[number::3]

        @pl.when(matrix == number)
        def _():
            for tile in range(4):
                for src, dst in ((st_ref, w_out), (m_ref, m_out), (v_ref, v_out)):
                    rows = W if src is st_ref else moment
                    for o in range(GROUP if src is st_ref else 1):
                        block = src.at[0, tile, 0, o] if src is st_ref else src.at[0, tile, 0]
                        if number == 2:
                            dst[0, o, tile] = block[...]
                        else:
                            for i in range(OWNERS):
                                dst[0, pl.ds(rows * o, rows), pl.ds(512 * i + W * tile, W)] = block[:, pl.ds(W * i, W)]


def run_lay_out(st, mo, vo):
    per = 2 * PARTS
    moment = W // PARTS

    def at(number, s):
        own = jnp.clip(s - number * per, 0, per - 1)
        return lax.div(own, PARTS), lax.rem(own, PARTS)

    def source(s):
        number, own = lax.div(s, per), lax.rem(s, per)
        return 1 - lax.div(own, PARTS), lax.rem(number + 1, 3), lax.rem(own, PARTS)

    def into(s):
        layer, matrix, part = source(s)
        return layer, 0, matrix, part, 0, 0

    def moments_into(s):
        layer, matrix, part = source(s)
        return layer, 0, matrix, part, 0

    like = jax.ShapeDtypeStruct
    specs, shapes = [], []
    for rows, kind in ((GROUP, BF16), (1, F32), (1, F32)):
        for number in range(3):
            height = W if kind == BF16 else moment
            if number == 2:
                block, whole = (1, rows, 4, height, D), (2, OWNERS if kind == BF16 else 1, 4, W, D)
                where = (lambda s: (*at(2, s), 0, 0, 0)) if kind == BF16 else (lambda s: (at(2, s)[0], 0, 0, at(2, s)[1], 0))
            else:
                block, whole = (1, rows * height, FF), (2, D if kind == BF16 else W, FF)
                where = functools.partial(lambda number, s: (*at(number, s), 0), number)
            specs.append(pl.BlockSpec(block, where))
            shapes.append(like(whole, kind))
    moments = pl.BlockSpec((1, 4, 1, moment, D), moments_into)
    out = pl.pallas_call(
        lay_out,
        name="lay_out",
        grid=(3 * per,),
        in_specs=[pl.BlockSpec((1, 4, 1, GROUP, W, D), into), moments, moments],
        out_specs=specs,
        out_shape=shapes,
        compiler_params=pltpu.CompilerParams(dimension_semantics=("arbitrary",), vmem_limit_bytes=VMEM_LIMIT),
    )(st, mo, vo)
    return [t.reshape(2, -1, t.shape[-1]) for t in out]


def solution(mesh):
    def step(x, dy, w_gate, w_up, w_down, m_gate, m_up, m_down, v_gate, v_up, v_down):
        x, dy = x[0], dy[0]
        st, mo, vo, *_ = run_main(x, dy, w_gate, w_up, w_down, m_gate, m_up, m_down, v_gate, v_up, v_down)
        st = st.reshape(2, 4, 3, OWNERS, W, D)
        mo, vo = (t.reshape(2, 4, 3, W, D) for t in (mo, vo))
        return tuple(run_lay_out(st, mo, vo))

    rows = P(None, "dp", None)
    sequences = P(("rep", "dp"), None, None)
    return jax.shard_map(
        step,
        mesh=mesh,
        in_specs=(sequences, sequences, *[P(None, None, None)] * 3, *[rows] * 6),
        out_specs=(*[P("rep", None, None)] * 3, *[P("rep", "dp", None)] * 6),
        check_vma=False,
    )
```

time: 725 us -> 715 us (0.986)
  Pallas kernels: 724 us -> 714 us
    pallas_call x1, Pallas kernels: 676 us -> 666 us  [run_main(): pl.pallas_call(main, name='main', in_specs=[any_spec] * len(args), out_sp...]
where the time goes in v2:
time: 715 us
  Pallas kernels  714 us (100%)
    pallas_call x1, Pallas kernels, run_main(): pl.pallas_call(main, name='main', in_specs=[any_spec] * len(args), out_sp...  666 us
    pallas_call x1, Pallas kernels, run_lay_out(): pl.pallas_call(lay_out, name='lay_out', grid=(3 * per,), in_specs=[pl.Blo...  48.4 us

profile of v2, /device:TPU:0, one launch (start us, length us, event | category | flops | bytes accessed | tf_op | source)
XLA Modules:
  0.0 714.6 jit_solution(1898393467080832189)
XLA Ops:
  0.6 665.5 %main.1 = (bf16[24,8,128,1024]{3,2,1,0:T(8,128)(2,1)}, f32[24,128,1024]{2,1,0:T(8,128)}, f32[24,128,1024]{2,1,0:T(8,128)}, bf16[24,4,128,1024]{3,2,1,0:T(8,128)(...) custom-call(bf16[2048,1024]{1,0:T(8,128)(2,1)} %bitcast.12, ...), custom_call_target="tpu_custom_call" | custom-call | flops 292057776128 | bytes 629145600 | tf_op jit(solution)/shard_map/main/pallas_call | solution.py:525
  666.2 48.4 %lay_out.1 = (bf16[2,1024,4096]{2,1,0:T(8,128)(2,1)}, bf16[2,1024,4096]{2,1,0:T(8,128)(2,1)}, bf16[2,8,4,128,1024]{4,3,2,1,0:T(8,128)(2,1)}, f32[2,128,4096]{2,1...) custom-call(bf16[2,4,3,8,128,1024]{5,4,3,2,1,0:T(8,128)(2,1)} %bitca, ...), custom_call_target="tpu_custom_call" | custom-call | tf_op jit(solution)/shard_map/lay_out/pallas_call | solution.py:596

commit v3 on v2

--- a/solution.py
+++ b/solution.py
@@ -17,13 +17,15 @@
 STEPS = 24
 TILES = 8
 VMEM_LIMIT = 63 << 20
+HOPS = (1, 2, 3)
 WAYS = (0, 1)
 ALONG = ((1,), (1,))
 F32, BF16 = jnp.float32, jnp.bfloat16
-SUMS = ((10, 16, 20, 12), (13, 21, 24, 18), (19, 26, 32, 22))
-STEP = (23, 35, 38, 29)
-GATHERS = ((30, 43, 45, 36), (39, 48, 50, 41), (50, 55, 58, 48))
-LAST = GATHERS[2][3] + 8 * (UNITS - 1)
+EARLY = 4
+SUMS = ((10, 16, 22, 38, 12), (13, 20, 26, 43, 18), (19, 25, 33, 48, 24))
+STEP = (23, 30, 41, 53, 30)
+GATHERS = ((28, 38, 48, 59, 37), (39, 44, 52, 67, 42), (46, 51, 62, 73, 51))
+LAST = GATHERS[2][EARLY] + 8 * (UNITS - 1)
 
 
 def normed(wide):
@@ -191,27 +193,25 @@
     def results(u):
         slot = u & 1
         here = st.at[u, me]
+        out = [remote(n_w.at[slot], here, n_sem.at[slot, way], ag_sem.at[way, u, 0], ahead[way]) for way in WAYS]
+        twin = remote(n_w.at[slot], here, n_sem.at[slot, 2], d_recv.at[u], partner)
+        stay = ((n_w, here), (n_m, mo.at[u]), (n_v, vo.at[u]))
+        return out, twin, [copy(new.at[slot], to, n_sem.at[slot, 3 + i]) for i, (new, to) in enumerate(stay)]
+
+    def results_start(u):
+        out, twin, stay = results(u)
         for way in WAYS:
-            yield ends[way] >= 1, remote(n_w.at[slot], here, n_sem.at[slot, way], ag_sem.at[way, u, 0], ahead[way])
-        yield None, remote(n_w.at[slot], here, n_sem.at[slot, 2], d_recv.at[u], partner)
-        yield None, copy(n_w.at[slot], here, n_sem.at[slot, 3])
-        yield None, copy(n_m.at[slot], mo.at[u], n_sem.at[slot, 4])
-        yield None, copy(n_v.at[slot], vo.at[u], n_sem.at[slot, 5])
-
-    def results_start(u):
-        for condition, c in results(u):
-            if condition is None:
-                c.start()
-            else:
-                pl.when(condition)(c.start)
+            pl.when(ends[way] >= 1)(out[way].start)
+        for c in (twin, *stay):
+            c.start()
 
     def results_wait(u):
-        for number, (condition, c) in enumerate(results(u)):
-            wait = c.wait_send if number < 3 else c.wait
-            if condition is None:
-                wait()
-            else:
-                pl.when(condition)(wait)
+        out, twin, stay = results(u)
+        for way in WAYS:
+            pl.when(ends[way] >= 1)(out[way].wait_send)
+        twin.wait_send()
+        for c in stay:
+            c.wait()
 
     def step_finish(u):
         @pl.when(u >= 2)
@@ -285,24 +285,25 @@
 
                 across(way, hop, u).start()
 
-    def turn(when, b, later, what, *args):
-        late = when[3] + later
-        u = jnp.where((b & 7 == late % 8) & (b >= late + 24), (b >> 3) - late // 8, -1)
-        for early in range(3):
-            u = jnp.where(b == when[early] + later, early, u)
+    def turn(when, b, what, *args):
+        late = when[EARLY]
+        u = jnp.where((b & 7 == late % 8) & (b >= late + 8 * EARLY), (b >> 3) - late // 8, -1)
+        for early in range(EARLY):
+            u = jnp.where(b == when[early], early, u)
         pl.when(live(u))(lambda: what(u, *args))
 
     def links(b):
-        for hop in (1, 2, 3):
-            turn(SUMS[hop - 1], b, 1, sum_finish, hop)
-        turn(STEP, b, 1, step_finish)
-        turn(SUMS[1], b, 0, sum_begin, 2)
-        turn(GATHERS[2], b, 0, gather, 4)
-        turn(SUMS[0], b, 0, sum_begin, 1)
-        turn(SUMS[2], b, 0, sum_begin, 3)
-        turn(GATHERS[1], b, 0, gather, 3)
-        turn(GATHERS[0], b, 0, gather, 2)
-        turn(STEP, b, 0, step_begin)
+        before = b - 1
+        for hop in HOPS:
+            turn(SUMS[hop - 1], before, sum_finish, hop)
+        turn(STEP, before, step_finish)
+        turn(STEP, b, step_begin)
+        turn(GATHERS[0], b, gather, 2)
+        turn(GATHERS[2], b, gather, 4)
+        turn(SUMS[1], b, sum_begin, 2)
+        turn(GATHERS[1], b, gather, 3)
+        turn(SUMS[2], b, sum_begin, 3)
+        turn(SUMS[0], b, sum_begin, 1)
 
 
     def stage_copies(n):
@@ -429,60 +430,76 @@
     lax.fori_loop(0, 4, first, 0)
     stage_wait(2)
 
-    def body(t, carry):
-        tile, k = lax.div(t, STEPS), lax.rem(t, STEPS)
-        slot = lax.rem(tile, 2)
-
-        @pl.when(k == 0)
+    def body(tile, carry):
+        slot = tile & 1
+        begun = jnp.where(tile == 0, 1, 0)
+        step = tile * STEPS
+        chunks = tile * 12
+
+        def steps(first, start, end, what):
+            def one(i, carry):
+                what(i)
+                links(step + first + i)
+                return carry
+
+            lax.fori_loop(start, end, one, 0)
+
+        @pl.when(tile > 0)
         def _():
             weights_wait(slot)
 
-            @pl.when(tile == 4)
-            def _():
-                copy(x_hbm, a_v, big_sem.at[0]).wait()
-                for c in range(4):
-                    a_v[chunk(c), :] = normed(a_v[chunk(c), :].astype(F32))
-
-        @pl.when(k < 8)
-        def _():
-            hidden(chunk(lax.div(k, 2)), chunk(lax.rem(k, 2)), slot)
-
-        pl.when(((k == 8) & (tile < 7)) | (t == 12))(
-            lambda: weights_in(1 - lax.div(tile + 1, 4), lax.rem(tile + 1, 4), 1 - slot)
-        )
-
-        for matrix in range(3):
-            pl.when((k >= 8 + 4 * matrix) & (k < 12 + 4 * matrix))(
-                functools.partial(gradient, tile, matrix, k - 8 - 4 * matrix)
-            )
-
-        pl.when((k == 20) & (tile == 3))(copy(x_hbm, a_v, big_sem.at[0]).start)
-
-        @pl.when((k >= 20) & (tile < 4))
-        def _():
-            rows = chunk(k - 20)
-            da_v[rows, :] += dot(dg_v[rows, :], wg_v[slot], ALONG) + dot(du_v[rows, :], wu_v[slot], ALONG)
-
-        @pl.when((k >= 20) & (tile == 3))
-        def _():
-            @pl.loop(0, 4)
-            def _(r):
-                rows = pl.ds(pl.multiple_of((k - 20) * 512 + r * W, W), W)
-                wide = h_v[rows, :].astype(F32)
-                da = da_v[rows, :].astype(BF16).astype(F32)
-                scale = lax.rsqrt(jnp.mean(wide * wide, -1, keepdims=True) + 1e-6)
-                along = jnp.sum(da * wide, -1, keepdims=True) * (scale * scale * scale) * (1.0 / D)
-                dh = (da * scale - wide * along).astype(BF16)
-                dy_v[rows, :] = (dy_v[rows, :].astype(F32) + dh.astype(F32)).astype(BF16)
-
-        @pl.when((k >= 9) & (k < 21))
-        def _():
-            stage_wait(jnp.where(t == 12, 1, 12 * tile + k - 9))
-
-        links(t)
+        @pl.when(tile == 4)
+        def _():
+            copy(x_hbm, a_v, big_sem.at[0]).wait()
+            for c in range(4):
+                a_v[chunk(c), :] = normed(a_v[chunk(c), :].astype(F32))
+
+        steps(0, begun * 8, 8, lambda i: hidden(chunk(i >> 1), chunk(i & 1), slot))
+
+        @pl.when(tile < TILES - 1)
+        def _():
+            weights_in(1 - ((tile + 1) >> 2), (tile + 1) & 3, 1 - slot)
+
+        def down(q):
+            gradient(tile, 0, q)
+            pl.when(q > 0)(lambda: stage_wait(chunks + q - 1))
+
+        def gate(q):
+            gradient(tile, 1, q)
+            stage_wait(jnp.where(tile + q == 0, 1, chunks + q + 3))
+
+        def up(q):
+            gradient(tile, 2, q)
+            stage_wait(chunks + q + 7)
+
+        def inner(c):
+            @pl.when(tile < 4)
+            def _():
+                rows = chunk(c)
+                da_v[rows, :] += dot(dg_v[rows, :], wg_v[slot], ALONG) + dot(du_v[rows, :], wu_v[slot], ALONG)
+
+            @pl.when(tile == 3)
+            def _():
+                @pl.loop(0, 4)
+                def _(r):
+                    rows = pl.ds(pl.multiple_of(c * 512 + r * W, W), W)
+                    wide = h_v[rows, :].astype(F32)
+                    da = da_v[rows, :].astype(BF16).astype(F32)
+                    scale = lax.rsqrt(jnp.mean(wide * wide, -1, keepdims=True) + 1e-6)
+                    along = jnp.sum(da * wide, -1, keepdims=True) * (scale * scale * scale) * (1.0 / D)
+                    dh = (da * scale - wide * along).astype(BF16)
+                    dy_v[rows, :] = (dy_v[rows, :].astype(F32) + dh.astype(F32)).astype(BF16)
+
+            pl.when(c == 0)(lambda: stage_wait(chunks + 11))
+
+        steps(8, begun * 4, 4, down)
+        steps(12, 0, 4, gate)
+        steps(16, 0, 4, up)
+        pl.when(tile == 3)(copy(x_hbm, a_v, big_sem.at[0]).start)
+        steps(20, 0, 4, inner)
         return carry
 
-    lax.fori_loop(12, TILES * STEPS, body, 0)
+    lax.fori_loop(0, TILES, body, 0)
 
     def rest(b, carry):
         links(b)
@@ -492,7 +509,7 @@
 
     last = UNITS - 1
     for way in WAYS:
-        for hop in (1, 2, 3):
+        for hop in HOPS:
             pl.when(sends(way, hop))(sum_out(way, hop, last).wait_send)
         for hop in (2, 3, 4):
 
@@ -613,12 +630,12 @@
         mo, vo = (t.reshape(2, 4, 3, W, D) for t in (mo, vo))
         return tuple(run_lay_out(st, mo, vo))
 
-    rows = P(None, "dp", None)
-    sequences = P(("rep", "dp"), None, None)
+    rows = P(None, "dp")
+    sequences = P(("rep", "dp"))
     return jax.shard_map(
         step,
         mesh=mesh,
-        in_specs=(sequences, sequences, *[P(None, None, None)] * 3, *[rows] * 6),
-        out_specs=(*[P("rep", None, None)] * 3, *[P("rep", "dp", None)] * 6),
+        in_specs=(sequences, sequences, *[P()] * 3, *[rows] * 6),
+        out_specs=(*[P("rep")] * 3, *[P("rep", "dp")] * 6),
         check_vma=False,
     )

time: 715 us -> 707 us (0.989)
  Pallas kernels: 714 us -> 705 us
    pallas_call x1, Pallas kernels: 666 us -> 657 us  [run_main(): pl.pallas_call(main, name='main', in_specs=[any_spec] * len(args), out_sp...]
where the time goes in v3:
time: 707 us; the launch traced here: 706 us
  Pallas kernels  705 us (100%)
    pallas_call x1, Pallas kernels, run_main(): pl.pallas_call(main, name='main', in_specs=[any_spec] * len(args), out_sp...  657 us
    pallas_call x1, Pallas kernels, run_lay_out(): pl.pallas_call(lay_out, name='lay_out', grid=(3 * per,), in_specs=[pl.Blo...  48.4 us

profile of v3, /device:TPU:0, one launch (start us, length us, event | category | flops | bytes accessed | tf_op | source)
XLA Modules:
  0.0 706.0 jit_solution(4820623043059827533)
XLA Ops:
  0.6 656.9 %main.1 = (bf16[24,8,128,1024]{3,2,1,0:T(8,128)(2,1)}, f32[24,128,1024]{2,1,0:T(8,128)}, f32[24,128,1024]{2,1,0:T(8,128)}, bf16[24,4,128,1024]{3,2,1,0:T(8,128)(...) custom-call(bf16[2048,1024]{1,0:T(8,128)(2,1)} %bitcast.12, ...), custom_call_target="tpu_custom_call" | custom-call | flops 292057776128 | bytes 629145600 | tf_op jit(solution)/shard_map/main/pallas_call | solution.py:542
  657.6 48.4 %lay_out.1 = (bf16[2,1024,4096]{2,1,0:T(8,128)(2,1)}, bf16[2,1024,4096]{2,1,0:T(8,128)(2,1)}, bf16[2,8,4,128,1024]{4,3,2,1,0:T(8,128)(2,1)}, f32[2,128,4096]{2,1...) custom-call(bf16[2,4,3,8,128,1024]{5,4,3,2,1,0:T(8,128)(2,1)} %bitca, ...), custom_call_target="tpu_custom_call" | custom-call | tf_op jit(solution)/shard_map/lay_out/pallas_call | solution.py:613
